TPU v7x, 32 devices: a whole 2x2x4 slice. The times are simulated.
32 devices in a mesh: dp: 8 (over z, x), ep: 4 (over y, core).
Axes of the slice: x: 2, y: 2, z: 4, core: 2. Of those that a mesh axis runs over, the one named last changes fastest.
Arguments:
- tokens: bfloat16 [64, 197, 768], P(('dp', 'ep')), may hold values from -6 to 6
- live_images: int32 [32], P(('dp', 'ep')), may hold values from 1 to 2, as said below
- routes: int32 [64, 197, 2], P(('dp', 'ep')), may hold values from 0 to 3, all different within a row; in each aligned block of 394 rows (0 to 393, 394 to 787, ..., all dimensions but the last counted through in order) at most 248 rows name the same one
- ln1_gain: float32 [768], replicated, may hold values from 0.1 to 1.9
- ln1_bias: float32 [768], replicated, may hold values from -3 to 3
- query_key_value_weight: bfloat16 [768, 2304], replicated, may hold values from -0.21875 to 0.21875
- attention_output_weight: bfloat16 [768, 768], replicated, may hold values from -0.625 to 0.625
- ln2_gain: float32 [768], replicated, may hold values from 0.1 to 1.9
- ln2_bias: float32 [768], replicated, may hold values from -3 to 3
- w_router: bfloat16 [768, 4], replicated, may hold values from -0.4375 to 0.4375
- w_in: bfloat16 [4, 768, 3072], P('ep'), may hold values from -0.21875 to 0.21875
- w_out: bfloat16 [4, 3072, 768], P('ep'), may hold values from -0.875 to 0.875
- cotangent: bfloat16 [64, 197, 768], P(('dp', 'ep')), may hold values from -6 to 6
Outputs:
- block_out: bfloat16 [64, 197, 768], P(('dp', 'ep'))
- grad_tokens: float32 [64, 197, 768], P(('dp', 'ep'))
- grad_ln1_gain: float32 [768], P('ep')
- grad_ln1_bias: float32 [768], P('ep')
- grad_w_qkv: float32 [768, 2304], P('ep')
- grad_w_attn_out: float32 [768, 768], P('ep')
- grad_ln2_gain: float32 [768], P('ep')
- grad_ln2_bias: float32 [768], P('ep')
- grad_w_router: float32 [768, 4], P('ep')
- grad_w_in: float32 [4, 768, 3072], P('ep', 'dp')
- grad_w_out: float32 [4, 3072, 768], P('ep', 'dp')
Inputs may be any that keep to these rules, and one draw needn't show every extreme that they name: Each device holds 2 image slots of which the first live_images are images; some device holds 2, some holds one. `routes`: each token names two different experts. Among the 394 tokens of one device, slots live or not, no expert is named more than 248 times, a bound that some block reaches.
All inputs are finite; a program needn't handle non-finite values.
Results may differ from a plain program's by a relative error of at most 0.024.
Values may be sent and summed in bfloat16 or wider, within the bound.
A program may use at most 192 MiB of HBM per device.

v0:
```python
import jax
import jax.numpy as jnp
from jax import lax
from jax.sharding import PartitionSpec as P

HEADS = 12
HEAD_DIM = 64
eps = 1e-06


def norm_forward(values):
    centre = jnp.mean(values, axis=-1, keepdims=True)
    shifted = values - centre
    inverse = lax.rsqrt(jnp.mean(shifted * shifted, axis=-1, keepdims=True) + eps)
    return (shifted * inverse, inverse)


def norm_backward(grad_normed, normalized_input, inverse):
    middle = jnp.mean(grad_normed, axis=-1, keepdims=True)
    along = jnp.mean(grad_normed * normalized_input, axis=-1, keepdims=True)
    return (grad_normed - middle - normalized_input * along) * inverse


def body(
    tokens,
    live_images,
    routes,
    ln1_gain,
    ln1_bias,
    query_key_value_weight,
    attention_output_weight,
    ln2_gain,
    ln2_bias,
    w_router,
    w_in,
    w_out,
    cotangent,
):
    slot_count, seq_len, model_width = tokens.shape
    row_count = slot_count * seq_len
    expert_count = w_router.shape[1]
    hidden_width = w_in.shape[2]
    capacity = ((2 * row_count + expert_count - 1) // expert_count * 5 // 4 + 7) // 8 * 8
    scaling = HEAD_DIM ** (-0.5)
    inputs = tokens.astype(jnp.float32).reshape(row_count, model_width)
    normed1, inverse1 = norm_forward(inputs)
    attn_in = (normed1 * ln1_gain + ln1_bias).astype(jnp.bfloat16)
    qkv_rows = jnp.dot(attn_in, query_key_value_weight, preferred_element_type=jnp.float32).astype(
        jnp.bfloat16
    )
    qkv_heads = qkv_rows.reshape(slot_count, seq_len, 3, HEADS, HEAD_DIM)
    queries = qkv_heads[:, :, 0]
    keys_all = qkv_heads[:, :, 1]
    values_all = qkv_heads[:, :, 2]
    scores = (
        jnp.einsum("sqhc,skhc->shqk", queries, keys_all, preferred_element_type=jnp.float32)
        * scaling
    )
    row_peak = jnp.max(scores, axis=-1, keepdims=True)
    raised = jnp.exp(scores - row_peak)
    totals = jnp.sum(raised, axis=-1, keepdims=True)
    log_total = row_peak + jnp.log(totals)
    weights = (raised / totals).astype(jnp.bfloat16)
    attended_context = jnp.einsum(
        "shqk,skhc->sqhc", weights, values_all, preferred_element_type=jnp.float32
    )
    attended_context = attended_context.astype(jnp.bfloat16).reshape(row_count, model_width)
    hidden1 = inputs + jnp.dot(
        attended_context, attention_output_weight, preferred_element_type=jnp.float32
    )
    normed2, inverse2 = norm_forward(hidden1)
    moe_in = (normed2 * ln2_gain + ln2_bias).astype(jnp.bfloat16)
    router = jax.nn.softmax(jnp.dot(moe_in, w_router, preferred_element_type=jnp.float32), axis=-1)
    chosen = routes.reshape(row_count, 2)
    expert_ids = jnp.arange(expert_count, dtype=jnp.int32)
    picked = (chosen[:, :, None] == expert_ids[None, None, :]).astype(jnp.float32)
    gates = jnp.sum(picked * router[:, None, :], axis=-1)
    token_live = (jnp.arange(row_count, dtype=jnp.int32) // seq_len < live_images[0]).astype(
        jnp.float32
    )
    pair_ids = chosen.reshape(2 * row_count)
    pair_live = jnp.repeat(token_live, 2) > 0.5
    member = ((pair_ids[:, None] == expert_ids[None, :]) & pair_live[:, None]).astype(jnp.int32)
    position = jnp.sum((jnp.cumsum(member, axis=0) - 1) * member, axis=-1)
    slot_ids = jnp.where(pair_live, pair_ids * capacity + position, -1).reshape(row_count, 2)
    lanes = jnp.arange(expert_count * capacity, dtype=jnp.int32)
    placing = (jnp.transpose(slot_ids)[:, None, :] == lanes[None, :, None]).astype(jnp.bfloat16)
    outbox = jnp.einsum("jsr,rd->sd", placing, moe_in, preferred_element_type=jnp.float32)
    outbox = outbox.astype(jnp.bfloat16).reshape(expert_count, capacity, model_width)
    inbox = lax.all_to_all(outbox, "ep", split_axis=0, concat_axis=0, tiled=True)
    flat_in = inbox.reshape(-1, model_width)
    pre_act = jnp.dot(flat_in, w_in[0], preferred_element_type=jnp.float32)
    activated = jax.nn.gelu(pre_act).astype(jnp.bfloat16)
    produced = jnp.dot(activated, w_out[0], preferred_element_type=jnp.float32).astype(jnp.bfloat16)
    coming_back = lax.all_to_all(
        produced.reshape(inbox.shape), "ep", split_axis=0, concat_axis=0, tiled=True
    )
    coming_back, pre_act = (
        coming_back,
        pre_act.reshape(inbox.shape[0], inbox.shape[1], hidden_width),
    )
    arrived_rows = inbox.reshape(-1, model_width)
    pre_rows = pre_act.reshape(-1, hidden_width)
    returned_rows = coming_back.reshape(expert_count * capacity, model_width)
    taken = jnp.einsum("jsr,sd->rjd", placing, returned_rows, preferred_element_type=jnp.float32)
    mixture = jnp.sum(gates[:, :, None] * taken, axis=1)
    block_out = (
        ((hidden1 + mixture) * token_live[:, None]).astype(jnp.bfloat16).reshape(tokens.shape)
    )
    upstream = cotangent.astype(jnp.float32).reshape(row_count, model_width) * token_live[:, None]
    gate_grads = jnp.sum(taken * upstream[:, None, :], axis=-1)
    sent_grads = (gates[:, :, None] * upstream[:, None, :]).astype(jnp.bfloat16)
    grad_outbox = jnp.einsum("jsr,rjd->sd", placing, sent_grads, preferred_element_type=jnp.float32)
    grad_outbox = grad_outbox.astype(jnp.bfloat16).reshape(expert_count, capacity, model_width)
    grad_inbox = lax.all_to_all(grad_outbox, "ep", split_axis=0, concat_axis=0, tiled=True)
    grad_rows = grad_inbox.reshape(-1, model_width)
    activated_rows, gelu_pull = jax.vjp(jax.nn.gelu, pre_rows)
    activated_low = activated_rows.astype(jnp.bfloat16)
    grad_activated = jnp.einsum(
        "rd,fd->rf", grad_rows, w_out[0], preferred_element_type=jnp.float32
    )
    grad_pre = gelu_pull(grad_activated)[0].astype(jnp.bfloat16)
    columns = activated_low
    grad_w_out = lax.psum_scatter(
        jnp.einsum("rf,rd->fd", columns, grad_rows, preferred_element_type=jnp.float32).astype(
            jnp.bfloat16
        ),
        "dp",
        scatter_dimension=0,
        tiled=True,
    ).astype(jnp.float32)
    grad_back_rows = jnp.einsum(
        "rf,df->rd", grad_pre, w_in[0], preferred_element_type=jnp.float32
    ).astype(jnp.bfloat16)
    grad_back = lax.all_to_all(
        grad_back_rows.reshape(grad_inbox.shape), "ep", split_axis=0, concat_axis=0, tiled=True
    )
    columns = arrived_rows
    grad_w_in = lax.psum_scatter(
        jnp.einsum("rd,rf->df", columns, grad_pre, preferred_element_type=jnp.float32).astype(
            jnp.bfloat16
        ),
        "dp",
        scatter_dimension=0,
        tiled=True,
    ).astype(jnp.float32)
    grad_back_flat = grad_back.reshape(expert_count * capacity, model_width)
    expert_grad = jnp.einsum(
        "jsr,sd->rd", placing, grad_back_flat, preferred_element_type=jnp.float32
    )
    grad_router_probs = jnp.sum(gate_grads[:, :, None] * picked, axis=1)
    grad_logits = router * (
        grad_router_probs - jnp.sum(router * grad_router_probs, axis=-1, keepdims=True)
    )
    grad_logits = grad_logits.astype(jnp.bfloat16)
    grad_w_router = jnp.einsum("rd,re->de", moe_in, grad_logits, preferred_element_type=jnp.float32)
    grad_moe_in = expert_grad + jnp.einsum(
        "re,de->rd", grad_logits, w_router, preferred_element_type=jnp.float32
    )
    grad_ln2_gain = jnp.sum(grad_moe_in * normed2, axis=0)
    grad_ln2_bias = jnp.sum(grad_moe_in, axis=0)
    grad_hidden1 = upstream + norm_backward(grad_moe_in * ln2_gain, normed2, inverse2)
    grad_attn = grad_hidden1.astype(jnp.bfloat16)
    grad_w_attn_out = jnp.einsum(
        "rd,re->de", attended_context, grad_attn, preferred_element_type=jnp.float32
    )
    grad_context = jnp.einsum(
        "re,de->rd", grad_attn, attention_output_weight, preferred_element_type=jnp.float32
    )
    grad_context = grad_context.astype(jnp.bfloat16).reshape(slot_count, seq_len, HEADS, HEAD_DIM)
    again = (
        jnp.einsum("sqhc,skhc->shqk", queries, keys_all, preferred_element_type=jnp.float32)
        * scaling
    )
    probs_again = jnp.exp(again - log_total)
    probs_low = probs_again.astype(jnp.bfloat16)
    grad_values = jnp.einsum(
        "shqk,sqhc->skhc", probs_low, grad_context, preferred_element_type=jnp.float32
    )
    grad_probs = jnp.einsum(
        "sqhc,skhc->shqk", grad_context, values_all, preferred_element_type=jnp.float32
    )
    grad_scores = probs_again * (
        grad_probs - jnp.sum(probs_again * grad_probs, axis=-1, keepdims=True)
    )
    grad_scores = grad_scores.astype(jnp.bfloat16)
    grad_queries = (
        jnp.einsum("shqk,skhc->sqhc", grad_scores, keys_all, preferred_element_type=jnp.float32)
        * scaling
    )
    grad_keys = (
        jnp.einsum("shqk,sqhc->skhc", grad_scores, queries, preferred_element_type=jnp.float32)
        * scaling
    )
    grad_qkv = (
        jnp.stack([grad_queries, grad_keys, grad_values], axis=2)
        .astype(jnp.bfloat16)
        .reshape(row_count, 3 * model_width)
    )
    grad_w_qkv = jnp.einsum("rd,re->de", attn_in, grad_qkv, preferred_element_type=jnp.float32)
    grad_attn_in = jnp.einsum(
        "re,de->rd", grad_qkv, query_key_value_weight, preferred_element_type=jnp.float32
    )
    grad_ln1_gain = jnp.sum(grad_attn_in * normed1, axis=0)
    grad_ln1_bias = jnp.sum(grad_attn_in, axis=0)
    grad_inputs = grad_hidden1 + norm_backward(grad_attn_in * ln1_gain, normed1, inverse1)
    shared = (
        grad_w_qkv,
        grad_w_attn_out,
        grad_w_router,
        grad_ln1_gain,
        grad_ln1_bias,
        grad_ln2_gain,
        grad_ln2_bias,
    )
    partial_sums = (
        lax.psum_scatter(
            shared[0].astype(jnp.bfloat16), "ep", scatter_dimension=0, tiled=True
        ).astype(jnp.float32),
        lax.psum_scatter(
            shared[1].astype(jnp.bfloat16), "ep", scatter_dimension=0, tiled=True
        ).astype(jnp.float32),
        lax.psum_scatter(
            shared[2].astype(jnp.bfloat16), "ep", scatter_dimension=0, tiled=True
        ).astype(jnp.float32),
        lax.psum_scatter(
            shared[3].astype(jnp.bfloat16), "ep", scatter_dimension=0, tiled=True
        ).astype(jnp.float32),
        lax.psum_scatter(
            shared[4].astype(jnp.bfloat16), "ep", scatter_dimension=0, tiled=True
        ).astype(jnp.float32),
        lax.psum_scatter(
            shared[5].astype(jnp.bfloat16), "ep", scatter_dimension=0, tiled=True
        ).astype(jnp.float32),
        lax.psum_scatter(
            shared[6].astype(jnp.bfloat16), "ep", scatter_dimension=0, tiled=True
        ).astype(jnp.float32),
    )
    shares = (
        lax.psum(partial_sums[0].astype(jnp.bfloat16), "dp").astype(jnp.float32),
        lax.psum(partial_sums[1].astype(jnp.bfloat16), "dp").astype(jnp.float32),
        lax.psum(partial_sums[2].astype(jnp.bfloat16), "dp").astype(jnp.float32),
        lax.psum(partial_sums[3].astype(jnp.bfloat16), "dp").astype(jnp.float32),
        lax.psum(partial_sums[4].astype(jnp.bfloat16), "dp").astype(jnp.float32),
        lax.psum(partial_sums[5].astype(jnp.bfloat16), "dp").astype(jnp.float32),
        lax.psum(partial_sums[6].astype(jnp.bfloat16), "dp").astype(jnp.float32),
    )
    return (
        block_out,
        grad_inputs.reshape(tokens.shape),
        shares[3],
        shares[4],
        shares[0],
        shares[1],
        shares[5],
        shares[6],
        shares[2],
        grad_w_in[None],
        grad_w_out[None],
    )


def solution(mesh):
    in_specs = (
        P(("dp", "ep"), None, None),
        P(("dp", "ep")),
        P(("dp", "ep"), None, None),
        P(),
        P(),
        P(),
        P(),
        P(),
        P(),
        P(),
        P("ep", None, None),
        P("ep", None, None),
        P(("dp", "ep"), None, None),
    )
    out_specs = (
        P(("dp", "ep"), None, None),
        P(("dp", "ep"), None, None),
        P("ep"),
        P("ep"),
        P("ep", None),
        P("ep", None),
        P("ep"),
        P("ep"),
        P("ep", None),
        P("ep", "dp", None),
        P("ep", "dp", None),
    )
    return jax.shard_map(body, mesh=mesh, in_specs=in_specs, out_specs=out_specs, check_vma=False)
```

profile of v0, /device:TPU:0, one launch (start us, length us, event | category | flops | bytes accessed | tf_op | source)
XLA Modules:
  0.0 590.4 jit_solution(2008736721865741235)
XLA Ops:
  40.4 4.2 convolution_convert_fusion.3
  44.6 6.6 %reshape.268 = bf16[2,197,3,12,64]{4,3,2,1,0:T(8,128)(2,1)} reshape(bf16[394,2304]{1,0:T(8,128)(2,1)} %convolution_convert_fusion.3) | data formatting | bytes 3631104 | tf_op jit(solution)/shard_map/reshape | solution.py:51
  51.3 5.0 fusion.71
  83.4 4.4 all-to-all-start
  97.5 3.7 bitcast_convert_fusion
  101.2 6.8 %all-to-all-done = bf16[4,248,768]{2,1,0:T(8,128)(2,1)} async-done(((bf16[4,248,768]{2,1,0:T(8,128)(2,1)}), bf16[4,248,768]{2,1,0:T(8,128)(2,1)}, u32[]{:S(2)}, u32[]{:S(2)}) %all-to-all-start) | async-done | bytes 1523744 | tf_op jit(solution)/shard_map/all_to_all | solution.py:90
  108.0 4.4 all-to-all-start.2
  112.4 7.2 %fusion.13 = f32[992,3072]{1,0:T(8,128)S(1)} fusion(bf16[992,768]{1,0:T(8,128)(2,1)} %bitcast.8, bf16[1,768,3072]{2,1,0:T(8,128)(2,1)} %param.23), kind=kOutput, calls=%fused_computation.25 | convolution fusion | flops 4680843264 | bytes 18432000 | tf_op jit(solution)/shard_map/dot_general | solution.py:92
  119.6 4.4 copy-done.56
  124.0 10.6 %fusion.32 = bf16[992,768]{1,0:T(8,128)(2,1)} fusion(bf16[1,3072,768]{2,1,0:T(8,128)(2,1)} %param.24, f32[992,3072]{1,0:T(8,128)S(1)} %fusion.13), kind=kOutput, calls=%fused_computation.48 | convolution fusion | flops 4709031936 | bytes 18432000 | tf_op jit(solution)/shard_map/dot_general | solution.py:94
  134.5 4.6 all-to-all-start.1
  139.1 14.9 %fusion.6 = bf16[992,3072]{1,0:T(8,128)(2,1)S(1)} fusion(f32[992,3072]{1,0:T(8,128)} %copy-done.56, bf16[992,768]{1,0:T(8,128)(2,1)} %bitcast.17, bf16[1,3072,768]{2,1,0:T(8,128)(2,1)} %param.24), kind=kOutput, calls=%fused_computation.8 | convolution fusion | flops 4741791744 | bytes 24526848 | tf_op jit(solution)/shard_map/rd,fd->rf/dot_general | solution.py:119
  156.6 8.3 %fusion.29 = bf16[992,768]{1,0:T(8,128)(2,1)} fusion(bf16[992,3072]{1,0:T(8,128)(2,1)S(1)} %fusion.6, bf16[1,768,3072]{2,1,0:T(8,128)(2,1)} %param.23), kind=kOutput, calls=%fused_computation.47 | convolution fusion | flops 4681605120 | bytes 12337152 | tf_op jit(solution)/shard_map/rf,df->rd/dot_general | solution.py:132
  165.0 4.5 all-to-all-start.3
  176.0 4.7 fusion.25
  181.4 7.6 %all-to-all-done.3 = bf16[4,248,768]{2,1,0:T(8,128)(2,1)} async-done(((bf16[4,248,768]{2,1,0:T(8,128)(2,1)}), bf16[4,248,768]{2,1,0:T(8,128)(2,1)}, u32[]{:S(2)}, u32[]{:S(2)}) %all-to-all-start.3) | async-done | bytes 1523744 | tf_op jit(solution)/shard_map/all_to_all | solution.py:135
  200.8 3.5 reshape.269
  207.3 4.7 multiply_reduce_fusion
  212.0 3.6 multiply_convert_fusion.1
  219.5 3.9 copy.137
  223.3 6.7 %convert_element_type.186 = bf16[394,2304]{0,1:T(8,128)(2,1)} reshape(bf16[2,197,3,12,64]{1,0,4,3,2:T(2,128)(2,1)} %copy.137) | data formatting | bytes 3631104 | tf_op jit(solution)/shard_map/convert_element_type | solution.py:197
  230.0 5.8 convolution_convert_fusion.2
  239.4 38.2 %reduce-scatter.8.cloned.1.call-done = bf16[192,2304]{1,0:T(8,128)(2,1)} async-done(((bf16[768,2304]{1,0:T(8,128)(2,1)}), bf16[192,2304]{1,0:T(8,128)(2,1)}) %reduce-scatter.8.cloned.1.call-update) | async-done | bytes 884752 | tf_op jit(solution)/shard_map/reduce_scatter | solution.py:217
  277.6 11.8 %convolution_convert_fusion = bf16[3072,768]{1,0:T(8,128)(2,1)} fusion(bf16[992,768]{1,0:T(8,128)(2,1)} %bitcast.17, f32[992,3072]{1,0:T(8,128)} %copy-done.56), kind=kOutput, calls=%fused_computation.10 | convolution fusion | flops 4710629376 | bytes 18432000 | tf_op jit(solution)/shard_map/rf,rd->fd/dot_general | solution.py:125
  289.5 9.1 %convolution_convert_fusion.1 = bf16[768,3072]{1,0:T(8,128)(2,1)} fusion(bf16[992,768]{1,0:T(8,128)(2,1)} %bitcast.8, bf16[992,3072]{1,0:T(8,128)(2,1)} %copy-done.55), kind=kOutput, calls=%fused_computation.11 | convolution fusion | flops 4683202560 | bytes 12337152 | tf_op jit(solution)/shard_map/rd,rf->df/dot_general | solution.py:140
  304.9 5.9 multiply_reduce_fusion.3
  310.8 6.8 %all-reduce.7 = (bf16[768]{0:T(1024)(128)(2,1)}, bf16[768]{0:T(1024)(128)(2,1)}, bf16[768]{0:T(1024)(128)(2,1)}, bf16[768]{0:T(1024)(128)(2,1)}) all-reduce(bf16[768]{0:T(1024)(128)(2,1)} %get-tuple-element.68, bf16[768]{0:T(1024)(128)(2,1)} %get-tuple-element.75, ...), channel_id=2, replica_groups=mesh['dp'=8,'ep'=4] {'ep'}, use_global_device_ids=true, to_apply=%region_23.24.clone | all-reduce | flops 3072 | bytes 12288
  323.5 3.5 multiply_add_fusion
  333.4 22.1 %all-reduce.5 = (bf16[192]{0:T(256)(128)(2,1)}, bf16[192]{0:T(256)(128)(2,1)}, bf16[192]{0:T(256)(128)(2,1)}, bf16[192]{0:T(256)(128)(2,1)}, bf16[192,4]{0,1:T(4,128)(2,1)S(1)}) all-reduce(bf16[192]{0:T(256)(128)(2,1)S(1)} %dynamic-slice.1, bf16[192]{0:T(256)(128)(2,1)S(1)} %copy-done.53, ...), channel_id=1, replica_groups=mesh['dp'=8,'ep'=4] {'dp'}, use_global_device_ids=true, to_apply=%region_24.25 | all-reduce | flops 1536 | bytes 6144 | tf_op jit(solution)/shard_map/psum | solution.py:243
  360.9 23.1 %all-reduce.10.cloned.1.call-done = (bf16[192,2304]{1,0:T(8,128)(2,1)}, bf16[192,768]{1,0:T(8,128)(2,1)}) async-done(((bf16[192,2304]{1,0:T(8,128)(2,1)}, bf16[192,768]{1,0:T(8,128)(2,1)}), (bf16[192,2304]{1,0:T(8,128)(2,1)}, bf16[192,768]{1,0:T(8,128)(2,1)})) %all-reduce.10.cloned.1.call-update) | async-done | bytes 1179664 | tf_op jit(solution)/shard_map/psum | solution.py:240
  388.4 94.0 %reduce-scatter.14.cloned.1.call-done = bf16[384,768]{1,0:T(8,128)(2,1)} async-done(((bf16[3072,768]{1,0:T(8,128)(2,1)}), bf16[384,768]{1,0:T(8,128)(2,1)}) %reduce-scatter.14.cloned.1.call-update) | async-done | bytes 589840 | tf_op jit(solution)/shard_map/reduce_scatter | solution.py:124
  484.5 96.7 %reduce-scatter.12.cloned.1.call-done = bf16[96,3072]{1,0:T(8,128)(2,1)} async-done(((bf16[768,3072]{1,0:T(8,128)(2,1)}), bf16[96,3072]{1,0:T(8,128)(2,1)}) %reduce-scatter.12.cloned.1.call-update) | async-done | bytes 589840 | tf_op jit(solution)/shard_map/reduce_scatter | solution.py:139
  (226 shorter events, 132.9 us)
Async XLA Ops:
  7.2 33.2 %copy-start = (bf16[768,2304]{1,0:T(8,128)(2,1)S(1)}, bf16[768,2304]{1,0:T(8,128)(2,1)}, u32[]{:S(2)}) copy-start(bf16[768,2304]{1,0:T(8,128)(2,1)} %param.18) | copy-start | bytes 10616836
  20.9 5.0 copy-start.42
  32.7 7.6 %copy-start.39 = (f32[768]{0:T(1024)S(1)}, f32[768]{0:T(1024)}, u32[]{:S(2)}) copy-start(f32[768]{0:T(1024)} %param.16) | copy-start | bytes 9220
  32.7 7.6 %copy-start.43 = (f32[394]{0:T(512)S(1)}, f32[394]{0:T(512)}, u32[]{:S(2)}) copy-start(f32[394]{0:T(512)} %div.53) | copy-start | bytes 4732
  32.8 7.6 %copy-start.45 = (f32[394]{0:T(512)S(1)}, f32[394]{0:T(512)}, u32[]{:S(2)}) copy-start(f32[394]{0:T(512)} %rsqrt.21) | copy-start | bytes 4732
  83.4 24.6 %all-to-all-start = ((bf16[4,248,768]{2,1,0:T(8,128)(2,1)}), bf16[4,248,768]{2,1,0:T(8,128)(2,1)}, u32[]{:S(2)}, u32[]{:S(2)}) async-start(bf16[4,248,768]{2,1,0:T(8,128)(2,1)} %bitcast.131), calls=%async_computation | async-start | bytes 3047424 | tf_op jit(solution)/shard_map/all_to_all | solution.py:90
  87.8 7.2 %copy-start.21 = (s32[394,2]{0,1:T(2,128)S(1)}, s32[394,2]{0,1:T(2,128)}, u32[]{:S(2)}) copy-start(s32[394,2]{0,1:T(2,128)} %eq.50) | copy-start | bytes 9460
  89.2 7.3 %copy-start.18 = (f32[394]{0:T(512)}, f32[394]{0:T(512)S(1)}, u32[]{:S(2)}) copy-start(f32[394]{0:T(512)S(1)} %get-tuple-element.96) | copy-start | bytes 4732
  108.0 26.5 %all-to-all-start.2 = ((bf16[4,248,768]{2,1,0:T(8,128)(2,1)}), bf16[4,248,768]{2,1,0:T(8,128)(2,1)}, u32[]{:S(2)}, u32[]{:S(2)}) async-start(bf16[4,248,768]{2,1,0:T(8,128)(2,1)} %bitcast.132), calls=%async_computation.2 | async-start | bytes 3047424 | tf_op jit(solution)/shard_map/all_to_all | solution.py:115
  119.6 4.4 copy-start.56
  134.5 30.4 %all-to-all-start.1 = ((bf16[4,248,768]{2,1,0:T(8,128)(2,1)}), bf16[4,248,768]{2,1,0:T(8,128)(2,1)}, u32[]{:S(2)}, u32[]{:S(2)}) async-start(bf16[4,248,768]{2,1,0:T(8,128)(2,1)} %bitcast.133), calls=%async_computation.1 | async-start | bytes 3047424 | tf_op jit(solution)/shard_map/all_to_all | solution.py:95
  165.0 4.5 copy-start.40
  165.0 24.1 %all-to-all-start.3 = ((bf16[4,248,768]{2,1,0:T(8,128)(2,1)}), bf16[4,248,768]{2,1,0:T(8,128)(2,1)}, u32[]{:S(2)}, u32[]{:S(2)}) async-start(bf16[4,248,768]{2,1,0:T(8,128)(2,1)} %bitcast.130), calls=%async_computation.3 | async-start | bytes 3047424 | tf_op jit(solution)/shard_map/all_to_all | solution.py:135
  169.4 6.6 %copy-start.38 = (s32[2,394]{1,0:T(2,128)S(1)}, s32[2,394]{1,0:T(2,128)}, u32[]{:S(2)}) copy-start(s32[2,394]{1,0:T(2,128)} %copy-done.36) | copy-start | bytes 9460
  169.5 69.9 %reduce-scatter.10.cloned.1.call-start = ((), (), s32[]{:S(2)}) async-start(), calls=%async_computation.10 | async-start | bytes 1474560 | tf_op jit(solution)/shard_map/reduce_scatter | solution.py:220
  171.7 4.3 copy-start.51
  176.0 4.7 copy-start.22
  176.0 4.7 copy-start.19
  176.0 4.7 copy-start.26
  200.8 76.8 %reduce-scatter.8.cloned.1.call-start = ((), (), s32[]{:S(2)}) async-start(), calls=%async_computation.9 | async-start | bytes 4423680 | tf_op jit(solution)/shard_map/reduce_scatter | solution.py:217
  207.3 4.7 copy-start.15
  207.3 10.1 %slice-start = ((s8[4915200]{0:T(1024)(128)(4,1)}), s8[4194304]{0:T(1024)(128)(4,1)S(1)}, s32[]{:S(2)}) async-start(s8[4915200]{0:T(1024)(128)(4,1)} %bitcast.128), calls=%async_computation.15 | async-start | bytes 8388608
  212.0 5.3 slice-start.1
  235.8 96.7 %reduce-scatter.16.cloned.1.call-start = ((), (), s32[]{:S(2)}) async-start(), calls=%async_computation.13 | async-start | bytes 245760
  239.3 144.8 %all-reduce.10.cloned.1.call-start = ((), (), s32[]{:S(2)}) async-start(), calls=%async_computation.14 | async-start | bytes 2359296 | tf_op jit(solution)/shard_map/psum | solution.py:240
  277.6 204.8 %reduce-scatter.14.cloned.1.call-start = ((), (), s32[]{:S(2)}) async-start(), calls=%async_computation.12 | async-start | bytes 5308416 | tf_op jit(solution)/shard_map/reduce_scatter | solution.py:124
  289.4 291.8 %reduce-scatter.12.cloned.1.call-start = ((), (), s32[]{:S(2)}) async-start(), calls=%async_computation.11 | async-start | bytes 5308416 | tf_op jit(solution)/shard_map/reduce_scatter | solution.py:139
  298.6 6.2 %copy-start.41 = (f32[768]{0:T(1024)S(1)}, f32[768]{0:T(1024)}, u32[]{:S(2)}) copy-start(f32[768]{0:T(1024)} %param.16) | copy-start | bytes 9220
  298.6 6.2 %copy-start.44 = (f32[394]{0:T(512)S(1)}, f32[394]{0:T(512)}, u32[]{:S(2)}) copy-start(f32[394]{0:T(512)} %div.53) | copy-start | bytes 4732
  298.7 6.2 %copy-start.46 = (f32[394]{0:T(512)S(1)}, f32[394]{0:T(512)}, u32[]{:S(2)}) copy-start(f32[394]{0:T(512)} %rsqrt.21) | copy-start | bytes 4732
  304.9 5.9 copy-start.47
  326.9 6.4 %copy-start.53 = (bf16[192]{0:T(256)(128)(2,1)S(1)}, bf16[192]{0:T(256)(128)(2,1)}, u32[]{:S(2)}) copy-start(bf16[192]{0:T(256)(128)(2,1)} %dynamic-slice.3) | copy-start | bytes 1156
  (37 other events, 72.9 us)
Sparse Core Ops, SparseCore 0:
  200.9 26.7 reduce-scatter.9
  235.9 41.5 reduce-scatter.7
  280.6 19.7 reduce-scatter.15
  303.8 80.2 all-reduce.9
  387.6 94.7 reduce-scatter.13
  485.9 95.3 reduce-scatter.11
where the time goes:
time: 596 us; the launch traced here: 590 us
  waiting for transfers between devices  267 us (45%)
  matrix products  114 us (19%)
  local copies, waits for them, and re-layouts  100 us (17%)
  other arithmetic  46.6 us (8%)
  blocking collectives  28.9 us (5%)
  starting transfers between devices  18 us (3%)
  between operations  16.4 us (3%)
    reduce_scatter x1, waiting for transfers between devices, body(): lax.psum_scatter(jnp.einsum('rd,rf->df', columns, grad_pre, preferred_ele...  96.7 us
    reduce_scatter x1, waiting for transfers between devices, body(): lax.psum_scatter(jnp.einsum('rf,rd->fd', columns, grad_rows, preferred_el...  94 us
    unnamed x135, local copies, waits for them, and re-layouts  41.7 us
    reduce_scatter x1, waiting for transfers between devices, body(): lax.psum_scatter(shared[0].astype(jnp.bfloat16), 'ep', scatter_dimension=...  38.2 us
    psum x1, waiting for transfers between devices, body(): lax.psum(partial_sums[0].astype(jnp.bfloat16), 'dp').astype(jnp.float32)  23.1 us
    psum x1, blocking collectives, body(): lax.psum(partial_sums[3].astype(jnp.bfloat16), 'dp').astype(jnp.float32)  22.1 us
    dot_general x1, matrix products, body(): jnp.einsum('rd,fd->rf', grad_rows, w_out[0], preferred_element_type=jnp.f...  14.9 us
  transfers between devices with their start and end apart: 10, of which 6 were waited for; matrix products, arithmetic and copies ran while one was open for 27% of the time, Pallas kernels for 0%

commit v1 on v0

--- a/solution.py
+++ b/solution.py
@@ -132,9 +132,20 @@
     grad_back_rows = jnp.einsum(
         "rf,df->rd", grad_pre, w_in[0], preferred_element_type=jnp.float32
     ).astype(jnp.bfloat16)
-    grad_back = lax.all_to_all(
-        grad_back_rows.reshape(grad_inbox.shape), "ep", split_axis=0, concat_axis=0, tiled=True
-    )
+    x = grad_back_rows.reshape(grad_inbox.shape)
+    ways, here = (lax.axis_size("ep"), lax.axis_index("ep"))
+    width = x.shape[0] // ways
+    dims = list(x.shape)
+    dims[0] = width
+    height = dims[0]
+    dims[0] = height * ways
+    full = jnp.zeros(dims, x.dtype)
+    for mask in range(ways):
+        part = lax.dynamic_slice_in_dim(x, (here ^ mask) * width, width, axis=0)
+        if mask:
+            part = lax.ppermute(part, "ep", [(d, d ^ mask) for d in range(ways)])
+        full = lax.dynamic_update_slice_in_dim(full, part, (here ^ mask) * height, axis=0)
+    grad_back = full
     columns = arrived_rows
     grad_w_in = lax.psum_scatter(
         jnp.einsum("rd,rf->df", columns, grad_pre, preferred_element_type=jnp.float32).astype(

time: 596 us -> 597 us (level)
  waiting for transfers between devices: 267 us -> 273 us
    ppermute x0 -> x3, waiting for transfers between devices: none -> 13.5 us  [body(): part = lax.ppermute(part, 'ep', [(d, d ^ mask) for d in range(ways)])]
    all_to_all x1 -> x0, waiting for transfers between devices: 7.64 us -> none  [body(): lax.all_to_all(grad_back_rows.reshape(grad_inbox.shape), 'ep', split_axis...]
    unnamed x135 -> x141, local copies, waits for them, and re-layouts: 41.7 us -> 37.8 us
  transfers between devices with their start and end apart: 10 -> 12, of which waited for: 6 -> 7; matrix products, arithmetic and copies ran while one was open for 27% -> 23% of each run, Pallas kernels for 0% -> 0%
where the time goes in v1:
time: 597 us; the launch traced here: 591 us
  waiting for transfers between devices  273 us (46%)
  matrix products  111 us (19%)
  local copies, waits for them, and re-layouts  100 us (17%)
  other arithmetic  43.9 us (7%)
  blocking collectives  28.9 us (5%)
  between operations  16.7 us (3%)
  starting transfers between devices  16.4 us (3%)
    reduce_scatter x1, waiting for transfers between devices, body(): lax.psum_scatter(jnp.einsum('rf,rd->fd', columns, grad_rows, preferred_el...  96.7 us
    reduce_scatter x1, waiting for transfers between devices, body(): lax.psum_scatter(jnp.einsum('rd,rf->df', columns, grad_pre, preferred_ele...  94.9 us
    reduce_scatter x1, waiting for transfers between devices, body(): lax.psum_scatter(shared[0].astype(jnp.bfloat16), 'ep', scatter_dimension=...  38.2 us
    unnamed x141, local copies, waits for them, and re-layouts  37.8 us
    psum x1, waiting for transfers between devices, body(): lax.psum(partial_sums[0].astype(jnp.bfloat16), 'dp').astype(jnp.float32)  23.1 us
    psum x1, blocking collectives, body(): lax.psum(partial_sums[3].astype(jnp.bfloat16), 'dp').astype(jnp.float32)  22.3 us
    dot_general x1, matrix products, body(): jnp.einsum('rd,fd->rf', grad_rows, w_out[0], preferred_element_type=jnp.f...  16.6 us
    ppermute x3, waiting for transfers between devices, body(): part = lax.ppermute(part, 'ep', [(d, d ^ mask) for d in range(ways)])  13.5 us
  transfers between devices with their start and end apart: 12, of which 7 were waited for; matrix products, arithmetic and copies ran while one was open for 23% of the time, Pallas kernels for 0%

profile of v1, /device:TPU:0, one launch (start us, length us, event | category | flops | bytes accessed | tf_op | source)
XLA Modules:
  0.0 590.8 jit_solution(8219124613068314517)
XLA Ops:
  22.2 4.3 convolution_convert_fusion.3
  26.5 6.8 %reshape.268 = bf16[2,197,3,12,64]{4,3,2,1,0:T(8,128)(2,1)} reshape(bf16[394,2304]{1,0:T(8,128)(2,1)} %convolution_convert_fusion.3) | data formatting | bytes 3631104 | tf_op jit(solution)/shard_map/reshape | solution.py:51
  33.3 5.0 fusion.71
  54.5 3.2 reshape.239
  81.7 4.8 all-to-all-start
  96.2 3.7 bitcast_convert_fusion
  99.9 6.8 %all-to-all-done = bf16[4,248,768]{2,1,0:T(8,128)(2,1)} async-done(((bf16[4,248,768]{2,1,0:T(8,128)(2,1)}), bf16[4,248,768]{2,1,0:T(8,128)(2,1)}, u32[]{:S(2)}, u32[]{:S(2)}) %all-to-all-start) | async-done | bytes 1523744 | tf_op jit(solution)/shard_map/all_to_all | solution.py:90
  106.7 4.3 all-to-all-start.2
  111.1 7.2 %fusion.13 = f32[992,3072]{1,0:T(8,128)S(1)} fusion(bf16[992,768]{1,0:T(8,128)(2,1)} %bitcast.8, bf16[1,768,3072]{2,1,0:T(8,128)(2,1)} %param.23), kind=kOutput, calls=%fused_computation.25 | convolution fusion | flops 4680843264 | bytes 18432000 | tf_op jit(solution)/shard_map/dot_general | solution.py:92
  118.3 4.5 copy-done.59
  122.8 10.5 %fusion.32 = bf16[992,768]{1,0:T(8,128)(2,1)} fusion(bf16[1,3072,768]{2,1,0:T(8,128)(2,1)} %param.24, f32[992,3072]{1,0:T(8,128)S(1)} %fusion.13), kind=kOutput, calls=%fused_computation.48 | convolution fusion | flops 4709031936 | bytes 18432000 | tf_op jit(solution)/shard_map/dot_general | solution.py:94
  133.3 16.6 %fusion.6 = bf16[992,3072]{1,0:T(8,128)(2,1)} fusion(f32[992,3072]{1,0:T(8,128)} %copy-done.59, bf16[992,768]{1,0:T(8,128)(2,1)} %bitcast.17, bf16[1,3072,768]{2,1,0:T(8,128)(2,1)} %param.24), kind=kOutput, calls=%fused_computation.8 | convolution fusion | flops 4741791744 | bytes 24526848 | tf_op jit(solution)/shard_map/rd,fd->rf/dot_general | solution.py:119
  149.8 4.3 all-to-all-start.1
  154.4 9.0 %fusion.29 = bf16[992,768]{1,0:T(8,128)(2,1)S(1)} fusion(bf16[992,3072]{1,0:T(8,128)(2,1)} %fusion.6, bf16[1,768,3072]{2,1,0:T(8,128)(2,1)} %param.23), kind=kOutput, calls=%fused_computation.47 | convolution fusion | flops 4681605120 | bytes 12337152 | tf_op jit(solution)/shard_map/rf,df->rd/dot_general | solution.py:132
  174.2 8.3 %collective-permute-done.1 = bf16[1,248,768]{2,1,0:T(8,128)(2,1)} collective-permute-done((bf16[1,248,768]{2,1,0:T(8,128)(2,1)}, bf16[1,248,768]{2,1,0:T(8,128)(2,1)}, u32[]{:S(2)}, u32[]{:S(2)}) %collective-permute-start.1) | collective-permute-done | bytes 380960 | tf_op jit(solution)/shard_map/ppermute | solution.py:146
  184.3 5.1 collective-permute-done.2
  190.3 3.9 fusion.25
  207.5 4.4 multiply_reduce_fusion
  212.0 3.8 multiply_convert_fusion.1
  219.6 3.9 copy.137
  223.5 6.5 %convert_element_type.186 = bf16[394,2304]{0,1:T(8,128)(2,1)} reshape(bf16[2,197,3,12,64]{1,0,4,3,2:T(2,128)(2,1)} %copy.137) | data formatting | bytes 3631104 | tf_op jit(solution)/shard_map/convert_element_type | solution.py:208
  230.1 5.8 convolution_convert_fusion.2
  239.4 38.2 %reduce-scatter.8.cloned.1.call-done = bf16[192,2304]{1,0:T(8,128)(2,1)} async-done(((bf16[768,2304]{1,0:T(8,128)(2,1)}), bf16[192,2304]{1,0:T(8,128)(2,1)}) %reduce-scatter.8.cloned.1.call-update) | async-done | bytes 884752 | tf_op jit(solution)/shard_map/reduce_scatter | solution.py:228
  277.9 9.1 %convolution_convert_fusion.1 = bf16[768,3072]{1,0:T(8,128)(2,1)} fusion(bf16[992,768]{1,0:T(8,128)(2,1)} %bitcast.8, bf16[992,3072]{1,0:T(8,128)(2,1)} %fusion.6), kind=kOutput, calls=%fused_computation.11 | convolution fusion | flops 4683202560 | bytes 12337152 | tf_op jit(solution)/shard_map/rd,rf->df/dot_general | solution.py:151
  287.1 11.8 %convolution_convert_fusion = bf16[3072,768]{1,0:T(8,128)(2,1)} fusion(bf16[992,768]{1,0:T(8,128)(2,1)} %bitcast.17, f32[992,3072]{1,0:T(8,128)} %copy-done.59), kind=kOutput, calls=%fused_computation.10 | convolution fusion | flops 4710629376 | bytes 18432000 | tf_op jit(solution)/shard_map/rf,rd->fd/dot_general | solution.py:125
  300.8 5.9 multiply_reduce_fusion.3
  306.7 6.5 %all-reduce.7 = (bf16[768]{0:T(1024)(128)(2,1)}, bf16[768]{0:T(1024)(128)(2,1)}, bf16[768]{0:T(1024)(128)(2,1)}, bf16[768]{0:T(1024)(128)(2,1)}) all-reduce(bf16[768]{0:T(1024)(128)(2,1)} %get-tuple-element.68, bf16[768]{0:T(1024)(128)(2,1)} %get-tuple-element.75, ...), channel_id=2, replica_groups=mesh['dp'=8,'ep'=4] {'ep'}, use_global_device_ids=true, to_apply=%region_23.24.clone | all-reduce | flops 3072 | bytes 12288
  319.0 3.5 multiply_add_fusion
  333.2 22.3 %all-reduce.5 = (bf16[192]{0:T(256)(128)(2,1)}, bf16[192]{0:T(256)(128)(2,1)}, bf16[192]{0:T(256)(128)(2,1)}, bf16[192]{0:T(256)(128)(2,1)}, bf16[192,4]{0,1:T(4,128)(2,1)S(1)}) all-reduce(bf16[192]{0:T(256)(128)(2,1)S(1)} %copy-done.56, bf16[192]{0:T(256)(128)(2,1)S(1)} %copy-done.57, ...), channel_id=1, replica_groups=mesh['dp'=8,'ep'=4] {'dp'}, use_global_device_ids=true, to_apply=%region_24.25 | all-reduce | flops 1536 | bytes 6144 | tf_op jit(solution)/shard_map/psum | solution.py:254
  361.0 23.1 %all-reduce.10.cloned.1.call-done = (bf16[192,2304]{1,0:T(8,128)(2,1)}, bf16[192,768]{1,0:T(8,128)(2,1)}) async-done(((bf16[192,2304]{1,0:T(8,128)(2,1)}, bf16[192,768]{1,0:T(8,128)(2,1)}), (bf16[192,2304]{1,0:T(8,128)(2,1)}, bf16[192,768]{1,0:T(8,128)(2,1)})) %all-reduce.10.cloned.1.call-update) | async-done | bytes 1179664 | tf_op jit(solution)/shard_map/psum | solution.py:251
  387.6 94.9 %reduce-scatter.12.cloned.1.call-done = bf16[96,3072]{1,0:T(8,128)(2,1)} async-done(((bf16[768,3072]{1,0:T(8,128)(2,1)}), bf16[96,3072]{1,0:T(8,128)(2,1)}) %reduce-scatter.12.cloned.1.call-update) | async-done | bytes 589840 | tf_op jit(solution)/shard_map/reduce_scatter | solution.py:150
  484.7 96.7 %reduce-scatter.14.cloned.1.call-done = bf16[384,768]{1,0:T(8,128)(2,1)} async-done(((bf16[3072,768]{1,0:T(8,128)(2,1)}), bf16[384,768]{1,0:T(8,128)(2,1)}) %reduce-scatter.14.cloned.1.call-update) | async-done | bytes 589840 | tf_op jit(solution)/shard_map/reduce_scatter | solution.py:124
  (241 shorter events, 129.3 us)
Async XLA Ops:
  7.2 15.0 %copy-start = (bf16[768,2304]{1,0:T(8,128)(2,1)S(1)}, bf16[768,2304]{1,0:T(8,128)(2,1)}, u32[]{:S(2)}) copy-start(bf16[768,2304]{1,0:T(8,128)(2,1)} %param.18) | copy-start | bytes 10616836
  9.0 6.7 %copy-start.42 = (s32[2,197,2]{1,2,0:T(2,128)S(1)}, s32[2,197,2]{1,2,0:T(2,128)}, u32[]{:S(2)}) copy-start(s32[2,197,2]{1,2,0:T(2,128)} %param.15) | copy-start | bytes 9460
  15.6 6.6 %copy-start.44 = (f32[768]{0:T(1024)S(1)}, f32[768]{0:T(1024)}, u32[]{:S(2)}) copy-start(f32[768]{0:T(1024)} %param.16) | copy-start | bytes 9220
  19.7 6.8 %copy-start.48 = (f32[394]{0:T(512)}, f32[394]{0:T(512)S(1)}, u32[]{:S(2)}) copy-start(f32[394]{0:T(512)S(1)} %rsqrt.21) | copy-start | bytes 4732
  19.8 6.7 %copy-start.50 = (f32[394]{0:T(512)}, f32[394]{0:T(512)S(1)}, u32[]{:S(2)}) copy-start(f32[394]{0:T(512)S(1)} %div.53) | copy-start | bytes 4732
  76.0 17.1 %copy-start.28 = (s32[394,2]{0,1:T(2,128)}, s32[394,2]{0,1:T(2,128)S(1)}, u32[]{:S(2)}) copy-start(s32[394,2]{0,1:T(2,128)S(1)} %eq.50) | copy-start | bytes 9460
  81.7 25.0 %all-to-all-start = ((bf16[4,248,768]{2,1,0:T(8,128)(2,1)}), bf16[4,248,768]{2,1,0:T(8,128)(2,1)}, u32[]{:S(2)}, u32[]{:S(2)}) async-start(bf16[4,248,768]{2,1,0:T(8,128)(2,1)} %bitcast.131), calls=%async_computation | async-start | bytes 3047424 | tf_op jit(solution)/shard_map/all_to_all | solution.py:90
  87.8 5.3 copy-start.26
  93.7 6.2 %copy-start.53 = (f32[394,2]{0,1:T(2,128)}, f32[394,2]{0,1:T(2,128)S(1)}, u32[]{:S(2)}) copy-start(f32[394,2]{0,1:T(2,128)S(1)} %select_reduce_fusion.1) | copy-start | bytes 9460
  106.7 26.5 %all-to-all-start.2 = ((bf16[4,248,768]{2,1,0:T(8,128)(2,1)}), bf16[4,248,768]{2,1,0:T(8,128)(2,1)}, u32[]{:S(2)}, u32[]{:S(2)}) async-start(bf16[4,248,768]{2,1,0:T(8,128)(2,1)} %bitcast.132), calls=%async_computation.2 | async-start | bytes 3047424 | tf_op jit(solution)/shard_map/all_to_all | solution.py:115
  118.3 4.5 copy-start.59
  149.8 40.4 %all-to-all-start.1 = ((bf16[4,248,768]{2,1,0:T(8,128)(2,1)}), bf16[4,248,768]{2,1,0:T(8,128)(2,1)}, u32[]{:S(2)}, u32[]{:S(2)}) async-start(bf16[4,248,768]{2,1,0:T(8,128)(2,1)} %bitcast.130), calls=%async_computation.1 | async-start | bytes 3047424 | tf_op jit(solution)/shard_map/all_to_all | solution.py:95
  154.2 85.3 %reduce-scatter.10.cloned.1.call-start = ((), (), s32[]{:S(2)}) async-start(), calls=%async_computation.9 | async-start | bytes 1474560 | tf_op jit(solution)/shard_map/reduce_scatter | solution.py:231
  164.6 7.8 %collective-permute-start = (bf16[1,248,768]{2,1,0:T(8,128)(2,1)}, bf16[1,248,768]{2,1,0:T(8,128)(2,1)}, u32[]{:S(2)}, u32[]{:S(2)}) collective-permute-start(bf16[1,248,768]{2,1,0:T(8,128)(2,1)} %get-tuple-element.92), channel_id=1, source_target_pairs={{0,1},{1,0},{2,3},{3,2},{4,5},{5,4},{6,7},{7,6},{8,9},{9,8},{10,11... | collective-permute-start | bytes 1142792 | tf_op jit(solution)/shard_map/ppermute | solution.py:146
  165.1 17.4 %collective-permute-start.1 = (bf16[1,248,768]{2,1,0:T(8,128)(2,1)}, bf16[1,248,768]{2,1,0:T(8,128)(2,1)}, u32[]{:S(2)}, u32[]{:S(2)}) collective-permute-start(bf16[1,248,768]{2,1,0:T(8,128)(2,1)} %get-tuple-element.91), channel_id=1, source_target_pairs={{0,2},{1,3},{2,0},{3,1},{4,6},{5,7},{6,4},{7,5},{8,10},{9,11},{10,... | collective-permute-start | bytes 1142792 | tf_op jit(solution)/shard_map/ppermute | solution.py:146
  168.9 21.3 %copy-start.41 = (s32[2,394]{1,0:T(2,128)S(1)}, s32[2,394]{1,0:T(2,128)}, u32[]{:S(2)}) copy-start(s32[2,394]{1,0:T(2,128)} %copy-done.39) | copy-start | bytes 9460
  168.9 21.3 %copy-start.54 = (f32[394,2]{0,1:T(2,128)S(1)}, f32[394,2]{0,1:T(2,128)}, u32[]{:S(2)}) copy-start(f32[394,2]{0,1:T(2,128)} %copy-done.53) | copy-start | bytes 9460
  171.0 18.5 %collective-permute-start.2 = (bf16[1,248,768]{2,1,0:T(8,128)(2,1)}, bf16[1,248,768]{2,1,0:T(8,128)(2,1)S(1)}, u32[]{:S(2)}, u32[]{:S(2)}) collective-permute-start(bf16[1,248,768]{2,1,0:T(8,128)(2,1)} %get-tuple-element.90), channel_id=1, source_target_pairs={{0,3},{1,2},{2,1},{3,0},{4,7},{5,6},{6,5},{7,4},{8,11},{9,10},{10,... | collective-permute-start | bytes 1142792 | tf_op jit(solution)/shard_map/ppermute | solution.py:146
  190.2 4.4 copy-start.3
  190.3 4.4 copy-start.17
  190.3 4.4 copy-start.21
  190.3 4.4 copy-start.34
  190.3 4.4 copy-start.36
  207.3 70.3 %reduce-scatter.8.cloned.1.call-start = ((), (), s32[]{:S(2)}) async-start(), calls=%async_computation.8 | async-start | bytes 4423680 | tf_op jit(solution)/shard_map/reduce_scatter | solution.py:228
  207.5 10.3 %slice-start = ((s8[4915200]{0:T(1024)(128)(4,1)}), s8[4194304]{0:T(1024)(128)(4,1)S(1)}, s32[]{:S(2)}) async-start(s8[4915200]{0:T(1024)(128)(4,1)} %bitcast.128), calls=%async_computation.14 | async-start | bytes 8388608
  212.0 5.9 slice-start.1
  235.9 96.5 %reduce-scatter.16.cloned.1.call-start = ((), (), s32[]{:S(2)}) async-start(), calls=%async_computation.12 | async-start | bytes 245760
  239.4 144.8 %all-reduce.10.cloned.1.call-start = ((), (), s32[]{:S(2)}) async-start(), calls=%async_computation.13 | async-start | bytes 2359296 | tf_op jit(solution)/shard_map/psum | solution.py:251
  277.6 204.9 %reduce-scatter.12.cloned.1.call-start = ((), (), s32[]{:S(2)}) async-start(), calls=%async_computation.10 | async-start | bytes 5308416 | tf_op jit(solution)/shard_map/reduce_scatter | solution.py:150
  287.1 294.3 %reduce-scatter.14.cloned.1.call-start = ((), (), s32[]{:S(2)}) async-start(), calls=%async_computation.11 | async-start | bytes 5308416 | tf_op jit(solution)/shard_map/reduce_scatter | solution.py:124
  327.9 5.3 copy-start.56
  327.9 5.3 copy-start.57
  (42 other events, 93.7 us)
Sparse Core Ops, SparseCore 0:
  207.4 26.8 reduce-scatter.9
  236.8 40.7 reduce-scatter.7
  280.6 19.7 reduce-scatter.15
  303.8 80.2 all-reduce.9
  387.7 94.7 reduce-scatter.11
  486.0 95.3 reduce-scatter.13
